TPU v7x, 32 devices: a whole 2x2x4 slice. The times are simulated.
32 devices in a mesh: rows: 8 (over z, x), cols: 4 (over y, core).
Axes of the slice: x: 2, y: 2, z: 4, core: 2. Of those that a mesh axis runs over, the one named last changes fastest.
Arguments:
- grad_out: bfloat16 [32, 512, 192], P(('rows', 'cols')), may hold values from -6 to 6
- inputs: bfloat16 [64, 1024, 192], P('rows', 'cols'), may hold values from -6 to 6
- weight: bfloat16 [3, 3, 192, 192], replicated, may hold values from -0.15625 to 0.15625
Outputs:
- input_grad: bfloat16 [64, 1024, 192], P('rows', 'cols')
- filter_grad: float32 [3, 3, 192, 192], replicated
All inputs are finite; a program needn't handle non-finite values.
Results may differ from a plain program's by a relative error of at most 0.0028.
Values may be sent and summed in bfloat16 or wider, within the bound.
A program may use at most 64 MiB of HBM per device.

v0:
```python
import math
import jax
import jax.numpy as jnp
from jax import lax
from jax.sharding import PartitionSpec as P


def shifted(x, axis, by):
    devices = lax.axis_size(axis)
    pairs = [(i, i + by) for i in range(devices) if 0 <= i + by < devices]
    return lax.ppermute(x, axis, pairs)


def tap_products(out_block, flat_weight):
    chans = flat_weight.shape[0]
    flat = out_block.reshape(-1, chans)
    products = jnp.dot(flat, flat_weight, preferred_element_type=jnp.float32)
    return products.reshape(out_block.shape[0], out_block.shape[1], 3, 3, chans)


def assemble(products, count_rows, count_cols):
    rows_even = products[:count_rows, :, 1]
    rows_odd = products[:count_rows, :, 2] + products[1 : count_rows + 1, :, 0]

    def columns(mixed):
        even = mixed[:, :count_cols, 1]
        odd = mixed[:, :count_cols, 2] + mixed[:, 1 : count_cols + 1, 0]
        return jnp.stack([even, odd], axis=2)

    placed = jnp.stack([columns(rows_even), columns(rows_odd)], axis=1)
    return placed.reshape(2 * count_rows, 2 * count_cols, products.shape[-1])


def filter_terms(input_band, out_band, row_taps):
    count_rows, count_cols, chans = out_band.shape
    split = input_band.reshape(count_rows + 1, 2, count_cols + 1, 2, chans)
    offsets = ((0, 0), (0, 1), (1, 0))
    pieces = []
    for row_tap in row_taps:
        start_row, parity_row = offsets[row_tap]
        for col_tap in range(3):
            start_col, parity_col = offsets[col_tap]
            pieces.append(
                split[
                    start_row : start_row + count_rows,
                    parity_row,
                    start_col : start_col + count_cols,
                    parity_col,
                ]
            )
    stacked = jnp.stack(pieces, axis=2).reshape(count_rows * count_cols, len(pieces) * chans)
    flat_out = out_band.reshape(count_rows * count_cols, chans)
    return lax.dot_general(
        stacked, flat_out, (((0,), (0,)), ((), ())), preferred_element_type=jnp.float32
    )


def per_device(grad_out, inputs, weight):
    chans = weight.shape[2]
    rows_local, cols_local = (inputs.shape[0], inputs.shape[1])
    half_rows, half_cols = (rows_local // 2, cols_local // 2)
    whole = lax.all_gather(grad_out, "cols", axis=0, tiled=True)
    out_grad = lax.dynamic_slice_in_dim(whole, lax.axis_index("cols") * half_cols, half_cols, 1)
    flat_weight = jnp.transpose(weight, (3, 0, 1, 2)).reshape(chans, 9 * chans)
    above = shifted(inputs[-1:], "rows", 1)
    with_above = jnp.concatenate([above, inputs], axis=0)
    left = shifted(with_above[:, -1:], "cols", 1)
    input_band = jnp.pad(jnp.concatenate([left, with_above], axis=1), ((0, 1), (0, 1), (0, 0)))
    positions = half_rows * lax.axis_size("rows") * (half_cols * lax.axis_size("cols"))
    scale = 1.0 / math.sqrt(positions)
    buckets = []
    for row_tap in range(3):
        terms = filter_terms(input_band, out_grad, (row_tap,))
        buckets.append(lax.psum(terms, ("rows", "cols")))
    summed = jnp.concatenate(buckets, axis=0)
    filter_grad = summed.reshape(3, 3, chans, chans) * scale
    framed = jnp.pad(out_grad, ((1, 1), (1, 1), (0, 0)))
    placed = assemble(tap_products(framed, flat_weight), half_rows + 1, half_cols + 1)
    extended = placed[1:, 1:]
    below = shifted(extended[:1].astype(jnp.bfloat16), "rows", -1).astype(jnp.float32)
    own_rows = extended[1:].at[-1].add(below[0])
    right = shifted(own_rows[:, :1], "cols", -1)
    input_grad = own_rows[:, 1:].at[:, -1].add(right[:, 0])
    return (input_grad.astype(jnp.bfloat16), filter_grad)


def solution(mesh):
    in_specs = (P(("rows", "cols"), None, None), P("rows", "cols", None), P())
    out_specs = (P("rows", "cols", None), P())
    return jax.shard_map(
        per_device, mesh=mesh, in_specs=in_specs, out_specs=out_specs, check_vma=False
    )
```

profile of v0, /device:TPU:0, one launch (start us, length us, event | category | flops | bytes accessed | tf_op | source)
XLA Modules:
  0.0 208.3 jit_solution(10896684272660905231)
XLA Ops:
  8.2 4.9 %collective-permute-start.2 = (bf16[1,256,192]{1,2,0:T(8,128)(2,1)S(1)}, bf16[1,256,192]{1,2,0:T(8,128)(2,1)S(1)}, u32[]{:S(2)}, u32[]{:S(2)}) collective-permute-start(bf16[1,256,192]{1,2,0:T(8,128)(2,1)S(1)} %slice.137), channel_id=1, source_target_pairs={{0,4},{4,8},{8,12},{12,16},{16,20},{20,24},{24,28},{1,5},{5,9},{9,... | collective-permute-start | bytes 294920 | tf_op jit(solution)/shard_map/ppermute | solution.py:11
  13.1 8.8 %all_gather.3 = bf16[4,512,192]{1,2,0:T(8,128)(2,1)S(1)} all-gather(bf16[1,512,192]{1,2,0:T(8,128)(2,1)} %param.7), channel_id=1, replica_groups=mesh['rows'=8,'cols'=4] {'cols'}, dimensions={0}, use_global_device_ids=true | all-gather | bytes 983040 | tf_op jit(solution)/shard_map/all_gather | solution.py:62
  25.7 2.5 %collective-permute-start.3 = (bf16[9,1,192]{1,2,0:T(8,128)(2,1)S(1)}, bf16[9,1,192]{1,2,0:T(8,128)(2,1)S(1)}, u32[]{:S(2)}, u32[]{:S(2)}) collective-permute-start(bf16[9,1,192]{1,2,0:T(8,128)(2,1)S(1)} %slice.163), channel_id=1, source_target_pairs={{0,1},{1,2},{2,3},{4,5},{5,6},{6,7},{8,9},{9,10},{10,11},{12,13},{... | collective-permute-start | bytes 10376 | tf_op jit(solution)/shard_map/ppermute | solution.py:11
  28.2 1.3 maximum_bitcast_fusion
  30.1 1.7 copy.92
  31.8 2.6 %pad.13.clone = bf16[10,258,192]{2,1,0:T(8,128)(2,1)} pad(bf16[9,257,192]{2,1,0:T(8,128)(2,1)} %copy.92, bf16[]{:T(256)} %constant.66.clone.1), padding=0_1x0_1x0_0 | pad | bytes 1878914 | tf_op jit(solution)/shard_map/jit(_pad)/pad | solution.py:68
  34.3 3.1 %reshape.97 = bf16[5,2,129,2,192]{4,3,2,1,0:T(2,128)(2,1)S(1)} reshape(bf16[10,258,192]{2,1,0:T(8,128)(2,1)} %pad.13.clone) | data formatting | bytes 1981440 | tf_op jit(solution)/shard_map/reshape | solution.py:36
  37.5 4.5 %fusion.18 = (bf16[4,1,128,1,192]{4,3,2,1,0:T(2,128)(2,1)S(1)}, bf16[4,1,128,1,192]{4,3,2,1,0:T(2,128)(2,1)}, bf16[4,1,128,1,192]{4,3,2,1,0:T(2,128)(2,1)S(1)}, ...) fusion(bf16[5,2,129,2,192]{4,3,2,1,0:T(2,128)(2,1)S(1)} %reshape.97), kind=kLoop, calls=%fused_computation.36 | loop fusion | bytes 3538944 | tf_op jit(solution)/shard_map/slice | solution.py:44
  43.2 1.2 copy.76
  44.4 1.3 copy.75
  46.3 1.2 copy.81
  47.5 1.9 copy.80
  57.1 1.5 pad_maximum_fusion
  58.6 1.4 copy.73
  60.0 2.9 %reshape.96 = f32[10,258,192]{2,1,0:T(8,128)} reshape(f32[5,2,129,2,192]{4,3,2,1,0:T(2,128)S(1)} %copy.73) | data formatting | bytes 3962880 | tf_op jit(solution)/shard_map/reshape | solution.py:31
  63.9 1.3 collective-permute-start
  65.2 1.8 slice.157
  67.0 4.9 %collective-permute-done = bf16[1,257,192]{2,1,0:T(8,128)(2,1)S(1)} collective-permute-done((bf16[1,257,192]{2,1,0:T(8,128)(2,1)S(1)}, bf16[1,257,192]{2,1,0:T(8,128)(2,1)S(1)}, u32[]{:S(2)}, u32[]{:S(2)}) %collective-permute-start) | collective-permute-done | bytes 98720 | tf_op jit(solution)/shard_map/ppermute | solution.py:11
  72.8 1.3 collective-permute-start.1
  74.4 4.1 %collective-permute-done.1 = f32[8,1,192]{2,1,0:T(1,128)S(1)} collective-permute-done((f32[8,1,192]{2,1,0:T(1,128)S(1)}, f32[8,1,192]{2,1,0:T(1,128)S(1)}, u32[]{:S(2)}, u32[]{:S(2)}) %collective-permute-start.1) | collective-permute-done | bytes 6176 | tf_op jit(solution)/shard_map/ppermute | solution.py:11
  78.5 1.3 copy.88
  79.8 115.7 %all-reduce.5.cloned.1.call-done = (f32[576,192]{0,1:T(8,128)}, f32[576,192]{0,1:T(8,128)}, f32[576,192]{0,1:T(8,128)}) async-done(((f32[576,192]{0,1:T(8,128)}, f32[576,192]{0,1:T(8,128)}, f32[576,192]{0,1:T(8,128)}), (f32[576,192]{0,1:T(8,128)}, f32[576,192]{0,1:T(8,128)}, f32[576,192]{0,1:T(8,128)})) %all-reduce.5.cloned.1.call-update) | async-done | bytes 1327120 | tf_op jit(solution)/shard_map/psum | solution.py:74
  195.5 1.6 concatenate.15
  198.4 3.1 %copy.87 = f32[1728,192]{1,0:T(8,128)} copy(f32[1728,192]{0,1:T(8,128)} %broadcast_multiply_fusion) | data formatting | bytes 2654208 | tf_op jit(solution)/shard_map/mul | solution.py:76
  (46 shorter events, 18.2 us)
Async XLA Ops:
  7.2 14.9 %copy-start = (bf16[3,3,192,192]{3,2,1,0:T(8,128)(2,1)S(1)}, bf16[3,3,192,192]{3,2,1,0:T(8,128)(2,1)}, u32[]{:S(2)}) copy-start(bf16[3,3,192,192]{3,2,1,0:T(8,128)(2,1)} %param.9) | copy-start | bytes 1990660
  7.2 188.3 %all-reduce.5.cloned.1.call-start = ((), (), s32[]{:S(2)}) async-start(), calls=%async_computation | async-start | bytes 2949120 | tf_op jit(solution)/shard_map/psum | solution.py:74
  8.2 17.2 %collective-permute-start.2 = (bf16[1,256,192]{1,2,0:T(8,128)(2,1)S(1)}, bf16[1,256,192]{1,2,0:T(8,128)(2,1)S(1)}, u32[]{:S(2)}, u32[]{:S(2)}) collective-permute-start(bf16[1,256,192]{1,2,0:T(8,128)(2,1)S(1)} %slice.137), channel_id=1, source_target_pairs={{0,4},{4,8},{8,12},{12,16},{16,20},{20,24},{24,28},{1,5},{5,9},{9,... | collective-permute-start | bytes 294920 | tf_op jit(solution)/shard_map/ppermute | solution.py:11
  24.1 1.3 copy-start.4
  25.7 3.7 %collective-permute-start.3 = (bf16[9,1,192]{1,2,0:T(8,128)(2,1)S(1)}, bf16[9,1,192]{1,2,0:T(8,128)(2,1)S(1)}, u32[]{:S(2)}, u32[]{:S(2)}) collective-permute-start(bf16[9,1,192]{1,2,0:T(8,128)(2,1)S(1)} %slice.163), channel_id=1, source_target_pairs={{0,1},{1,2},{2,3},{4,5},{5,6},{6,7},{8,9},{9,10},{10,11},{12,13},{... | collective-permute-start | bytes 10376 | tf_op jit(solution)/shard_map/ppermute | solution.py:11
  44.4 5.0 %copy-start.3 = (bf16[4,1,128,1,192]{4,3,2,1,0:T(2,128)(2,1)S(1)}, bf16[4,1,128,1,192]{4,3,2,1,0:T(2,128)(2,1)}, u32[]{:S(2)}) copy-start(bf16[4,1,128,1,192]{4,3,2,1,0:T(2,128)(2,1)} %get-tuple-element.50) | copy-start | bytes 589828
  51.4 2.8 %copy-start.2 = (bf16[4,1,128,1,192]{4,3,2,1,0:T(2,128)(2,1)S(1)}, bf16[4,1,128,1,192]{4,3,2,1,0:T(2,128)(2,1)}, u32[]{:S(2)}) copy-start(bf16[4,1,128,1,192]{4,3,2,1,0:T(2,128)(2,1)} %get-tuple-element.46) | copy-start | bytes 589828
  55.4 1.7 copy-start.1
  63.9 7.9 %collective-permute-start = (bf16[1,257,192]{2,1,0:T(8,128)(2,1)S(1)}, bf16[1,257,192]{2,1,0:T(8,128)(2,1)S(1)}, u32[]{:S(2)}, u32[]{:S(2)}) collective-permute-start(bf16[1,257,192]{2,1,0:T(8,128)(2,1)S(1)} %slice.187), channel_id=1, source_target_pairs={{4,0},{8,4},{12,8},{16,12},{20,16},{24,20},{28,24},{5,1},{9,5},{13... | collective-permute-start | bytes 296072 | tf_op jit(solution)/shard_map/ppermute | solution.py:11
  72.8 5.6 %collective-permute-start.1 = (f32[8,1,192]{2,1,0:T(1,128)S(1)}, f32[8,1,192]{2,1,0:T(1,128)S(1)}, u32[]{:S(2)}, u32[]{:S(2)}) collective-permute-start(f32[8,1,192]{2,1,0:T(1,128)S(1)} %slice.162), channel_id=1, source_target_pairs={{1,0},{2,1},{3,2},{5,4},{6,5},{7,6},{9,8},{10,9},{11,10},{13,12},{... | collective-permute-start | bytes 18440 | tf_op jit(solution)/shard_map/ppermute | solution.py:11
Sparse Core Ops, SparseCore 0:
  57.2 138.2 all-reduce.4
where the time goes:
time: 209 us; the launch traced here: 208 us
  waiting for transfers between devices  125 us (60%)
  local copies, waits for them, and re-layouts  36.9 us (18%)
  between operations  14.3 us (7%)
  starting transfers between devices  9.95 us (5%)
  other arithmetic  8.95 us (4%)
  blocking collectives  8.84 us (4%)
  matrix products  4.68 us (2%)
    psum x1, waiting for transfers between devices, per_device(): buckets.append(lax.psum(terms, ('rows', 'cols')))  116 us
    slice x10, local copies, waits for them, and re-layouts, filter_terms(): split[start_row:start_row + count_rows, parity_row, start_col:start_col +...  13.3 us
    ppermute x4, starting transfers between devices, shifted(): return lax.ppermute(x, axis, pairs)  9.91 us
    ppermute x4, waiting for transfers between devices, shifted(): return lax.ppermute(x, axis, pairs)  8.96 us
    all_gather x1, blocking collectives, per_device(): whole = lax.all_gather(grad_out, 'cols', axis=0, tiled=True)  8.84 us
  transfers between devices with their start and end apart: 5, of which 3 were waited for; matrix products, arithmetic and copies ran while one was open for 8% of the time, Pallas kernels for 0%

commit v1 on v0

--- a/solution.py
+++ b/solution.py
@@ -3,6 +3,12 @@
 import jax.numpy as jnp
 from jax import lax
 from jax.sharding import PartitionSpec as P
+
+
+def add_all(block, axis):
+    shards = lax.all_gather(block, axis, axis=0, tiled=False)
+    total = shards.sum(axis=0)
+    return total
 
 
 def shifted(x, axis, by):
@@ -71,7 +77,7 @@
     buckets = []
     for row_tap in range(3):
         terms = filter_terms(input_band, out_grad, (row_tap,))
-        buckets.append(lax.psum(terms, ("rows", "cols")))
+        buckets.append(add_all(terms, ("rows", "cols")))
     summed = jnp.concatenate(buckets, axis=0)
     filter_grad = summed.reshape(3, 3, chans, chans) * scale
     framed = jnp.pad(out_grad, ((1, 1), (1, 1), (0, 0)))

time: 209 us -> 403 us (1.93)
  waiting for transfers between devices: 125 us -> 303 us
  other arithmetic: 8.95 us -> 26.3 us
    all_gather x0 -> x3, waiting for transfers between devices: none -> 294 us  [add_all(): shards = lax.all_gather(block, axis, axis=0, tiled=False)]
    psum x1 -> x0, waiting for transfers between devices: 116 us -> none  [per_device(): buckets.append(lax.psum(terms, ('rows', 'cols')))]
    reduce_sum x0 -> x3, other arithmetic: none -> 19 us  [add_all(): total = shards.sum(axis=0)]
  transfers between devices with their start and end apart: 5 -> 7, of which waited for: 3 -> 6; matrix products, arithmetic and copies ran while one was open for 8% -> 8% of each run, Pallas kernels for 0% -> 0%
where the time goes in v1:
time: 403 us; the launch traced here: 402 us
  waiting for transfers between devices  303 us (75%)
  local copies, waits for them, and re-layouts  34.3 us (9%)
  other arithmetic  26.3 us (7%)
  between operations  14.1 us (3%)
  starting transfers between devices  10.8 us (3%)
  blocking collectives  8.84 us (2%)
  matrix products  4.66 us (1%)
    all_gather x3, waiting for transfers between devices, add_all(): shards = lax.all_gather(block, axis, axis=0, tiled=False)  294 us
    reduce_sum x3, other arithmetic, add_all(): total = shards.sum(axis=0)  19 us
    slice x10, local copies, waits for them, and re-layouts, filter_terms(): split[start_row:start_row + count_rows, parity_row, start_col:start_col +...  11.8 us
    ppermute x4, starting transfers between devices, shifted(): return lax.ppermute(x, axis, pairs)  10.5 us
    ppermute x4, waiting for transfers between devices, shifted(): return lax.ppermute(x, axis, pairs)  8.95 us
    all_gather x1, blocking collectives, per_device(): whole = lax.all_gather(grad_out, 'cols', axis=0, tiled=True)  8.84 us
  transfers between devices with their start and end apart: 7, of which 6 were waited for; matrix products, arithmetic and copies ran while one was open for 8% of the time, Pallas kernels for 0%

profile of v1, /device:TPU:0, one launch (start us, length us, event | category | flops | bytes accessed | tf_op | source)
XLA Modules:
  0.0 402.1 jit_solution(6410907812230691960)
XLA Ops:
  8.2 4.9 %collective-permute-start.2 = (bf16[1,256,192]{1,2,0:T(8,128)(2,1)S(1)}, bf16[1,256,192]{1,2,0:T(8,128)(2,1)S(1)}, u32[]{:S(2)}, u32[]{:S(2)}) collective-permute-start(bf16[1,256,192]{1,2,0:T(8,128)(2,1)S(1)} %slice.137), channel_id=1, source_target_pairs={{0,4},{4,8},{8,12},{12,16},{16,20},{20,24},{24,28},{1,5},{5,9},{9,... | collective-permute-start | bytes 294920 | tf_op jit(solution)/shard_map/ppermute | solution.py:17
  13.1 8.8 %all_gather.21 = bf16[4,512,192]{1,2,0:T(8,128)(2,1)S(1)} all-gather(bf16[1,512,192]{1,2,0:T(8,128)(2,1)} %param.7), channel_id=1, replica_groups=mesh['rows'=8,'cols'=4] {'cols'}, dimensions={0}, use_global_device_ids=true | all-gather | bytes 983040 | tf_op jit(solution)/shard_map/all_gather | solution.py:68
  23.3 3.0 collective-permute-start.3
  27.1 2.7 pad_maximum_fusion.1
  29.8 2.1 copy.106
  31.9 1.3 pad.13.clone
  33.1 3.1 reshape.97
  36.3 4.4 %fusion.15 = (bf16[4,1,128,1,192]{4,3,2,1,0:T(2,128)(2,1)}, bf16[4,1,128,1,192]{4,3,2,1,0:T(2,128)(2,1)}, bf16[4,1,128,1,192]{4,3,2,1,0:T(2,128)(2,1)}, bf16[4,1...) fusion(bf16[5,2,129,2,192]{4,3,2,1,0:T(2,128)(2,1)S(1)} %reshape.97), kind=kLoop, calls=%fused_computation.36 | loop fusion | bytes 3538944 | tf_op jit(solution)/shard_map/slice | solution.py:50
  42.0 1.2 copy.99
  57.1 1.4 copy.87
  58.5 2.9 reshape.96
  62.4 1.3 collective-permute-start
  63.7 1.8 slice.157
  65.5 3.8 collective-permute-done
  70.3 1.3 collective-permute-start.1
  71.9 4.5 %collective-permute-done.1 = f32[8,1,192]{2,1,0:T(1,128)S(1)} collective-permute-done((f32[8,1,192]{2,1,0:T(1,128)S(1)}, f32[8,1,192]{2,1,0:T(1,128)S(1)}, u32[]{:S(2)}, u32[]{:S(2)}) %collective-permute-start.1) | collective-permute-done | bytes 6176 | tf_op jit(solution)/shard_map/ppermute | solution.py:17
  76.5 1.3 copy.102
  77.7 84.7 %all-gather.14.cloned.1.call-done = f32[32,576,192]{1,2,0:T(8,128)} async-done(((f32[1,576,192]{1,2,0:T(8,128)}), f32[32,576,192]{1,2,0:T(8,128)}) %all-gather.14.cloned.1.call-update) | async-done | bytes 14155792 | tf_op jit(solution)/shard_map/all_gather | solution.py:9
  162.4 6.3 %reduce_sum.29 = f32[576,192]{0,1:T(8,128)S(1)} reduce(f32[32,576,192]{1,2,0:T(8,128)} %all-gather.14.cloned.1.call-done, f32[]{:T(128)} %constant.70.clone.1), dimensions={0}, to_apply=%region_2.3 | reduce | flops 3428352 | bytes 14598148 | tf_op jit(solution)/shard_map/reduce_sum | solution.py:10
  168.7 104.4 %all-gather.12.cloned.1.call-done = f32[32,576,192]{1,2,0:T(8,128)} async-done(((f32[1,576,192]{1,2,0:T(8,128)}), f32[32,576,192]{1,2,0:T(8,128)}) %all-gather.12.cloned.1.call-update) | async-done | bytes 14155792 | tf_op jit(solution)/shard_map/all_gather | solution.py:9
  273.2 6.3 %reduce_sum.28 = f32[576,192]{0,1:T(8,128)S(1)} reduce(f32[32,576,192]{1,2,0:T(8,128)} %all-gather.12.cloned.1.call-done, f32[]{:T(128)} %constant.70.clone.1), dimensions={0}, to_apply=%region_1.2 | reduce | flops 3428352 | bytes 14598148 | tf_op jit(solution)/shard_map/reduce_sum | solution.py:10
  279.5 105.0 %all-gather.10.cloned.1.call-done = f32[32,576,192]{1,2,0:T(8,128)} async-done(((f32[1,576,192]{1,2,0:T(8,128)}), f32[32,576,192]{1,2,0:T(8,128)}) %all-gather.10.cloned.1.call-update) | async-done | bytes 14155792 | tf_op jit(solution)/shard_map/all_gather | solution.py:9
  384.5 6.3 %reduce_sum.27 = f32[576,192]{0,1:T(8,128)S(1)} reduce(f32[32,576,192]{1,2,0:T(8,128)} %all-gather.10.cloned.1.call-done, f32[]{:T(128)} %constant.70.clone.1), dimensions={0}, to_apply=%region_0.1 | reduce | flops 3428352 | bytes 14598148 | tf_op jit(solution)/shard_map/reduce_sum | solution.py:10
  392.5 3.1 copy.101
  (55 shorter events, 22.0 us)
Async XLA Ops:
  7.2 47.4 %copy-start = (bf16[3,3,192,192]{3,2,1,0:T(8,128)(2,1)S(1)}, bf16[3,3,192,192]{3,2,1,0:T(8,128)(2,1)}, u32[]{:S(2)}) copy-start(bf16[3,3,192,192]{3,2,1,0:T(8,128)(2,1)} %param.9) | copy-start | bytes 1990660
  7.2 155.2 %all-gather.14.cloned.1.call-start = ((), (), s32[]{:S(2)}) async-start(), calls=%async_computation.2 | async-start | bytes 16220160 | tf_op jit(solution)/shard_map/all_gather | solution.py:9
  8.2 13.7 %collective-permute-start.2 = (bf16[1,256,192]{1,2,0:T(8,128)(2,1)S(1)}, bf16[1,256,192]{1,2,0:T(8,128)(2,1)S(1)}, u32[]{:S(2)}, u32[]{:S(2)}) collective-permute-start(bf16[1,256,192]{1,2,0:T(8,128)(2,1)S(1)} %slice.137), channel_id=1, source_target_pairs={{0,4},{4,8},{8,12},{12,16},{16,20},{20,24},{24,28},{1,5},{5,9},{9,... | collective-permute-start | bytes 294920 | tf_op jit(solution)/shard_map/ppermute | solution.py:17
  23.3 3.8 collective-permute-start.3
  44.5 3.0 copy-start.4
  44.5 3.9 copy-start.3
  46.2 227.0 %all-gather.12.cloned.1.call-start = ((), (), s32[]{:S(2)}) async-start(), calls=%async_computation.1 | async-start | bytes 16220160 | tf_op jit(solution)/shard_map/all_gather | solution.py:9
  48.8 3.0 copy-start.2
  51.5 332.9 %all-gather.10.cloned.1.call-start = ((), (), s32[]{:S(2)}) async-start(), calls=%async_computation | async-start | bytes 16220160 | tf_op jit(solution)/shard_map/all_gather | solution.py:9
  62.4 6.9 %collective-permute-start = (bf16[1,257,192]{2,1,0:T(8,128)(2,1)S(1)}, bf16[1,257,192]{2,1,0:T(8,128)(2,1)S(1)}, u32[]{:S(2)}, u32[]{:S(2)}) collective-permute-start(bf16[1,257,192]{2,1,0:T(8,128)(2,1)S(1)} %slice.187), channel_id=1, source_target_pairs={{4,0},{8,4},{12,8},{16,12},{20,16},{24,20},{28,24},{5,1},{9,5},{13... | collective-permute-start | bytes 296072 | tf_op jit(solution)/shard_map/ppermute | solution.py:17
  70.3 6.1 %collective-permute-start.1 = (f32[8,1,192]{2,1,0:T(1,128)S(1)}, f32[8,1,192]{2,1,0:T(1,128)S(1)}, u32[]{:S(2)}, u32[]{:S(2)}) collective-permute-start(f32[8,1,192]{2,1,0:T(1,128)S(1)} %slice.162), channel_id=1, source_target_pairs={{1,0},{2,1},{3,2},{5,4},{6,5},{7,6},{9,8},{10,9},{11,10},{13,12},{... | collective-permute-start | bytes 18440 | tf_op jit(solution)/shard_map/ppermute | solution.py:17
  391.3 4.3 %copy-start.1 = (bf16[3,3,192,192]{3,2,1,0:T(8,128)(2,1)S(1)}, bf16[3,3,192,192]{3,2,1,0:T(8,128)(2,1)}, u32[]{:S(2)}) copy-start(bf16[3,3,192,192]{3,2,1,0:T(8,128)(2,1)} %param.9) | copy-start | bytes 1990660
Sparse Core Ops, SparseCore 0:
  46.3 116.0 all-gather.13
  165.3 107.7 all-gather.11
  276.7 107.7 all-gather.9
